TPU v7x, 32 devices: a whole 2x2x4 slice. The times are simulated.
32 devices in a mesh: seq: 8 (over z, y), grp: 4 (over x, core).
Axes of the slice: x: 2, y: 2, z: 4, core: 2. Of those that a mesh axis runs over, the one named last changes fastest.
Arguments:
- query_nope: bfloat16 [4, 2, 128, 128], P(None, None, 'seq'), may hold values from -12.859821 to 12.859821
- query_rope: bfloat16 [4, 2, 128, 64], P(None, None, 'seq'), may hold values from -150 to 150
- latent_cache: bfloat16 [4, 8192, 576], P(None, ('seq', 'grp')), may hold values from -5 to 5
- lengths: int32 [4], replicated, may hold values from 4096 to 8192
- key_weight: bfloat16 [128, 128, 512], P('seq'), may hold values from -0.5 to 0.5
- value_weight: bfloat16 [128, 512, 128], P('seq'), may hold values from -0.25 to 0.25
- output_weight: bfloat16 [16384, 7168], P('seq', 'grp'), may hold values from -0.0625 to 0.0625
Outputs:
- mixed: bfloat16 [4, 2, 7168], P(None, None, ('grp', 'seq'))
All inputs are finite; a program needn't handle non-finite values.
Results may differ from a plain program's by a relative error of at most 0.0095.
Values may be sent and summed in bfloat16 or wider, within the bound.
No kernel may reach another device: no remote copies, remote signals or barrier semaphores. Data moves between devices by JAX's collectives and lax.ppermute only.
A program may use at most 64 MiB of HBM per device.

v0:
```python
import jax
import jax.numpy as jnp
from jax import lax
from jax.sharding import PartitionSpec as P

NEGATIVE = -1e30


def joined(part, axis, combine):
    gathered = jax.tree.map(lambda a: lax.all_gather(a, axis), part)

    def take(source):
        return jax.tree.map(lambda a: lax.dynamic_index_in_dim(a, source, 0, False), gathered)

    return lax.fori_loop(
        1, lax.axis_size(axis), lambda source, state: combine(state, take(source)), take(0)
    )


def shard_partial(queries, cache_block, limits, offset, factor, latent_width):
    raw_score = (
        jnp.einsum("bqhd,bpd->bqhp", queries, cache_block, preferred_element_type=jnp.float32)
        * factor
    )
    places = offset + lax.broadcasted_iota(jnp.int32, (1, 1, cache_block.shape[1]), 2)
    visible = places < limits[:, :, None]
    scores = jnp.where(visible[:, :, None, :], raw_score, NEGATIVE)
    maxima = jnp.max(scores, axis=-1)
    powers = jnp.exp(scores - maxima[..., None])
    totals = jnp.sum(powers, axis=-1)
    weights = powers.astype(jnp.bfloat16)
    summed = jnp.einsum(
        "bqhp,bpd->bqhd",
        weights,
        cache_block[:, :, :latent_width],
        preferred_element_type=jnp.float32,
    )
    return (maxima, totals, (summed / totals[..., None]).astype(jnp.bfloat16))


def merge_sources(partials, maxima, totals):
    highest = jnp.max(maxima, axis=0)
    shares = totals * jnp.exp(maxima - highest[None])
    summed = jnp.sum(shares, axis=0)
    numerator = jnp.sum(shares[..., None] * partials.astype(jnp.float32), axis=0)
    return (highest, summed, numerator / summed[..., None])


def merge_tuple(received):
    return merge_sources(received[0], received[1], received[2])


def join_pairs(earlier, later):
    highest = jnp.maximum(earlier[0], later[0])
    left_share = earlier[1] * jnp.exp(earlier[0] - highest)
    right_share = later[1] * jnp.exp(later[0] - highest)
    summed = left_share + right_share
    blended = (left_share[..., None] * earlier[2] + right_share[..., None] * later[2]) / summed[
        ..., None
    ]
    return (highest, summed, blended)


def absorb(query_nope, query_rope, key_weight):
    absorbed = jnp.einsum(
        "bqhn,hnd->bqhd", query_nope, key_weight, preferred_element_type=jnp.float32
    )
    return jnp.concatenate([absorbed.astype(jnp.bfloat16), query_rope], axis=-1)


def up_project(latent_out, value_weight):
    values = jnp.einsum(
        "bqhd,hde->bqhe", latent_out, value_weight, preferred_element_type=jnp.float32
    ).astype(jnp.bfloat16)
    return values.reshape(values.shape[0], values.shape[1], values.shape[2] * values.shape[3])


def shards(query_nope, query_rope, latent_cache, lengths, key_weight, value_weight, output_weight):
    latent_width = key_weight.shape[2]
    factor = float(query_nope.shape[3] + query_rope.shape[3]) ** (-0.5)
    positions = latent_cache.shape[1]
    drafts = query_nope.shape[1]
    offset = (lax.axis_index("seq") * lax.axis_size("grp") + lax.axis_index("grp")) * positions
    limits = lengths[:, None] - drafts + 1 + lax.broadcasted_iota(jnp.int32, (1, drafts), 1)
    own_queries = absorb(query_nope, query_rope, key_weight)
    maxima, totals, partials = shard_partial(
        lax.all_gather(own_queries, "seq", axis=2, tiled=True),
        latent_cache,
        limits,
        offset,
        factor,
        latent_width,
    )
    partials, maxima, totals = (partials, maxima, totals)
    sources = (partials[None], maxima[None], totals[None])
    gathered = merge_tuple(
        (
            lax.all_to_all(
                sources[0].astype(jnp.float32), "seq", split_axis=3, concat_axis=0, tiled=True
            ).astype(jnp.bfloat16),
            lax.all_to_all(sources[1], "seq", split_axis=3, concat_axis=0, tiled=True),
            lax.all_to_all(sources[2], "seq", split_axis=3, concat_axis=0, tiled=True),
        )
    )
    highest, summed, blended = joined((gathered[0], gathered[1], gathered[2]), "grp", join_pairs)
    values = up_project(blended.astype(jnp.bfloat16), value_weight)
    head_terms = jnp.dot(values, output_weight, preferred_element_type=jnp.float32)
    reduced = lax.psum_scatter(head_terms, "seq", scatter_dimension=2, tiled=True)
    return reduced.astype(jnp.bfloat16)


def solution(mesh):
    in_specs = (
        P(None, None, "seq", None),
        P(None, None, "seq", None),
        P(None, ("seq", "grp"), None),
        P(),
        P("seq", None, None),
        P("seq", None, None),
        P("seq", "grp"),
    )
    out_specs = P(None, None, ("grp", "seq"))
    return jax.shard_map(shards, mesh=mesh, in_specs=in_specs, out_specs=out_specs, check_vma=False)
```

profile of v0, /device:TPU:0, one launch (start us, length us, event | category | flops | bytes accessed | tf_op | source)
XLA Modules:
  0.0 212.3 jit_solution(17703678175560071938)
XLA Ops:
  6.5 0.9 copy.29
  8.1 1.1 fusion.18
  10.2 44.5 %all-gather.5.cloned.1.call-done = bf16[4,2,128,576]{3,0,1,2:T(4,128)(2,1)} async-done(((bf16[4,2,16,576]{3,0,1,2:T(4,128)(2,1)}), bf16[4,2,128,576]{3,0,1,2:T(4,128)(2,1)}) %all-gather.5.cloned.1.call-update) | async-done | bytes 1179664 | tf_op jit(solution)/shard_map/all_gather | solution.py:87
  54.7 2.4 %fusion.42 = (f32[4,2,128]{2,1,0:T(2,128)S(1)}, f32[4,2,128,256]{3,2,1,0:T(8,128)S(1)}) fusion(bf16[4,256,576]{1,2,0:T(8,128)(2,1)} %param.11, bf16[4,2,128,576]{3,0,1,2:T(4,128)(2,1)} %all-gather.5.cloned.1.call-done, pred[4,2,256]{2,1,0:T(4,128)(4,1)S(1)} %broadcast_compare_fusion), kind=kOutput, calls=%fused_computation.50 | convolution fusion | flops 302775296 | bytes 3414016 | tf_op jit(solution)/shard_map/bqhd,bpd->bqhp/dot_general | solution.py:22
  57.7 0.8 reshape.85
  58.5 3.4 %all-to-all-start.1 = ((f32[8,1,128]{2,1,0:T(1,128)}), f32[8,1,128]{2,1,0:T(1,128)S(1)}, u32[]{:S(2)}, u32[]{:S(2)}) async-start(f32[8,1,128]{2,1,0:T(1,128)} %reshape.85), calls=%async_computation.1 | async-start | bytes 8192 | tf_op jit(solution)/shard_map/all_to_all | solution.py:102
  62.9 5.5 %all-to-all-done.1 = f32[8,1,128]{2,1,0:T(1,128)S(1)} async-done(((f32[8,1,128]{2,1,0:T(1,128)}), f32[8,1,128]{2,1,0:T(1,128)S(1)}, u32[]{:S(2)}, u32[]{:S(2)}) %all-to-all-start.1) | async-done | bytes 4128 | tf_op jit(solution)/shard_map/all_to_all | solution.py:102
  68.4 3.3 %all-to-all-start = ((f32[8,1,128]{2,1,0:T(1,128)}), f32[8,1,128]{2,1,0:T(1,128)S(1)}, u32[]{:S(2)}, u32[]{:S(2)}) async-start(f32[8,1,128]{2,1,0:T(1,128)} %reshape.83), calls=%async_computation | async-start | bytes 8192 | tf_op jit(solution)/shard_map/all_to_all | solution.py:101
  71.7 1.7 fusion.11
  73.5 2.1 copy.38
  75.6 2.5 %all-to-all-done = f32[8,1,128]{2,1,0:T(1,128)S(1)} async-done(((f32[8,1,128]{2,1,0:T(1,128)}), f32[8,1,128]{2,1,0:T(1,128)S(1)}, u32[]{:S(2)}, u32[]{:S(2)}) %all-to-all-start) | async-done | bytes 4128 | tf_op jit(solution)/shard_map/all_to_all | solution.py:101
  78.1 3.6 %all-to-all-start.2 = ((bf16[1,4,2,128,512]{4,2,1,0,3:T(2,128)(2,1)}), bf16[1,4,2,128,512]{4,2,1,0,3:T(2,128)(2,1)S(1)}, u32[]{:S(2)}, u32[]{:S(2)}) async-start(bf16[1,4,2,128,512]{4,2,1,0,3:T(2,128)(2,1)} %copy.38), calls=%async_computation.2 | async-start | bytes 2097152 | tf_op jit(solution)/shard_map/all_to_all | solution.py:98
  83.1 1.6 copy.35
  85.6 0.9 copy.32
  86.6 1.8 fusion.40
  88.4 16.5 %all-to-all-done.2 = bf16[1,4,2,128,512]{4,2,1,0,3:T(2,128)(2,1)S(1)} async-done(((bf16[1,4,2,128,512]{4,2,1,0,3:T(2,128)(2,1)}), bf16[1,4,2,128,512]{4,2,1,0,3:T(2,128)(2,1)S(1)}, u32[]{:S(2)}, u32[]{:S(2)}) %all-to-all-start.2) | async-done | bytes 1048608 | tf_op jit(solution)/shard_map/all_to_all | solution.py:98
  104.9 2.3 %fusion.7 = f32[4,2,16,512]{3,1,0,2:T(2,128)S(1)} fusion(bf16[1,4,2,8,16,512]{5,2,1,4,3,0:T(2,128)(2,1)S(1)} %bitcast.108, f32[8,4,2,16]{2,1,3,0:T(4,128)} %get-tuple-element.201), kind=kLoop, calls=%fused_computation.13 | loop fusion | flops 1507328 | bytes 1314816 | tf_op jit(solution)/shard_map/reduce_sum | solution.py:45
  107.3 0.9 copy.39
  108.5 5.2 %all-gather.1 = f32[16,2,16]{2,1,0:T(2,128)S(1)} all-gather(f32[4,2,16]{2,1,0:T(2,128)S(1)} %copy.36), channel_id=3, replica_groups=mesh['seq'=8,'grp'=4] {'grp'}, dimensions={0}, use_global_device_ids=true | all-gather | bytes 2560 | tf_op jit(solution)/shard_map/all_gather | solution.py:10
  113.7 5.2 %all-gather = f32[16,2,16]{2,1,0:T(2,128)S(1)} all-gather(f32[4,2,16]{2,1,0:T(2,128)S(1)} %copy.33), channel_id=2, replica_groups=mesh['seq'=8,'grp'=4] {'grp'}, dimensions={0}, use_global_device_ids=true | all-gather | bytes 2560 | tf_op jit(solution)/shard_map/all_gather | solution.py:10
  118.9 5.1 %all-gather.7.cloned.1.call-done = f32[4,4,2,16,512]{4,3,2,1,0:T(8,128)} async-done(((f32[1,4,2,16,512]{4,3,2,1,0:T(8,128)}), f32[4,4,2,16,512]{4,3,2,1,0:T(8,128)}) %all-gather.7.cloned.1.call-update) | async-done | bytes 1048592 | tf_op jit(solution)/shard_map/all_gather | solution.py:10
  124.0 1.0 slice_bitcast_fusion
  124.9 3.5 %while.19 = (s32[]{:T(128)}, f32[4,2,16]{2,1,0:T(2,128)S(1)}, f32[4,2,16]{2,1,0:T(2,128)S(1)}, f32[4,2,16,512]{3,2,1,0:T(8,128)S(1)}, f32[4,4,2,16]{3,2,1,0:T(2,...) while((s32[]{:T(128)}, f32[4,2,16]{2,1,0:T(2,128)S(1)}, ...), condition=%wide.region_6.7_spmd, body=%wide.region_5.6_spmd.sunk | while | flops 262917 | bytes 792207 | solution.py:15
  125.0 1.1 fusion.46
  126.2 1.1 fusion.46
  127.3 1.1 fusion.46
  128.4 2.0 fusion.24
  130.5 4.2 %fusion.3 = f32[4,2,1792]{2,0,1:T(4,128)S(1)} fusion(bf16[2048,1792]{1,0:T(8,128)(2,1)} %param.15, bf16[16,2,1,4,128]{4,3,2,1,0:T(4,128)(2,1)S(1)} %fusion.24), kind=kOutput, calls=%fused_computation.8 | convolution fusion | flops 58720256 | bytes 7430144 | tf_op jit(solution)/shard_map/dot_general | solution.py:107
  134.7 2.3 %copy.49 = f32[4,2,1792]{0,1,2:T(2,128)} copy(f32[4,2,1792]{2,0,1:T(4,128)S(1)} %fusion.3) | data formatting | bytes 114688
  137.0 3.1 %reshape.81 = f32[1792,8]{1,0:T(8,128)} reshape(f32[1792,2,4]{2,1,0:T(2,128)} %bitcast.107) | data formatting | bytes 114688
  140.1 63.9 %reduce-scatter.4.cloned.1.call-done = f32[224,8]{1,0:T(8,128)} async-done(((f32[1792,8]{1,0:T(8,128)}), f32[224,8]{1,0:T(8,128)}) %reduce-scatter.4.cloned.1.call-update) | async-done | bytes 7184
  204.0 1.0 reshape.82
  (36 shorter events, 6.8 us)
Async XLA Ops:
  6.5 1.6 copy-start
  6.5 3.5 %copy-start.1 = (s32[4]{0:T(128)S(1)}, s32[4]{0:T(128)}, u32[]{:S(2)}) copy-start(s32[4]{0:T(128)} %param.12) | copy-start | bytes 52
  6.5 48.2 %all-gather.5.cloned.1.call-start = ((), (), s32[]{:S(2)}) async-start(), calls=%async_computation.4 | async-start | bytes 1474560 | tf_op jit(solution)/shard_map/all_gather | solution.py:87
  58.5 9.9 %all-to-all-start.1 = ((f32[8,1,128]{2,1,0:T(1,128)}), f32[8,1,128]{2,1,0:T(1,128)S(1)}, u32[]{:S(2)}, u32[]{:S(2)}) async-start(f32[8,1,128]{2,1,0:T(1,128)} %reshape.85), calls=%async_computation.1 | async-start | bytes 8192 | tf_op jit(solution)/shard_map/all_to_all | solution.py:102
  68.4 9.7 %all-to-all-start = ((f32[8,1,128]{2,1,0:T(1,128)}), f32[8,1,128]{2,1,0:T(1,128)S(1)}, u32[]{:S(2)}, u32[]{:S(2)}) async-start(f32[8,1,128]{2,1,0:T(1,128)} %reshape.83), calls=%async_computation | async-start | bytes 8192 | tf_op jit(solution)/shard_map/all_to_all | solution.py:101
  78.1 26.8 %all-to-all-start.2 = ((bf16[1,4,2,128,512]{4,2,1,0,3:T(2,128)(2,1)}), bf16[1,4,2,128,512]{4,2,1,0,3:T(2,128)(2,1)S(1)}, u32[]{:S(2)}, u32[]{:S(2)}) async-start(bf16[1,4,2,128,512]{4,2,1,0,3:T(2,128)(2,1)} %copy.38), calls=%async_computation.2 | async-start | bytes 2097152 | tf_op jit(solution)/shard_map/all_to_all | solution.py:98
  81.6 42.3 %all-gather.7.cloned.1.call-start = ((), (), s32[]{:S(2)}) async-start(), calls=%async_computation.5 | async-start | bytes 1310720 | tf_op jit(solution)/shard_map/all_gather | solution.py:10
  108.2 95.8 %reduce-scatter.4.cloned.1.call-start = ((), (), s32[]{:S(2)}) async-start(), calls=%async_computation.6 | async-start | bytes 1032192
Sparse Core Ops, SparseCore 0:
  10.2 44.5 all-gather.4
  108.4 15.5 all-gather.6
  140.3 63.6 reduce-scatter.3
where the time goes:
time: 213 us; the launch traced here: 212 us
  waiting for transfers between devices  138 us (65%)
  local copies, waits for them, and re-layouts  18.2 us (9%)
  between operations  13.3 us (6%)
  matrix products  11.5 us (5%)
  starting transfers between devices  10.4 us (5%)
  blocking collectives  10.4 us (5%)
  other arithmetic  10.3 us (5%)
    unnamed x4, waiting for transfers between devices  63.9 us
    all_gather x1, waiting for transfers between devices, shards(): lax.all_gather(own_queries, 'seq', axis=2, tiled=True)  44.5 us
    all_to_all x1, waiting for transfers between devices, shards(): lax.all_to_all(sources[0].astype(jnp.float32), 'seq', split_axis=3, conca...  16.5 us
    all_gather x2, blocking collectives, joined(): gathered = jax.tree.map(lambda a: lax.all_gather(a, axis), part)  10.4 us
    unnamed x13, local copies, waits for them, and re-layouts  10.2 us
    all_to_all x1, waiting for transfers between devices, shards(): lax.all_to_all(sources[2], 'seq', split_axis=3, concat_axis=0, tiled=True)  5.53 us
    all_gather x1, waiting for transfers between devices, joined(): gathered = jax.tree.map(lambda a: lax.all_gather(a, axis), part)  5.1 us
  transfers between devices with their start and end apart: 6, of which 6 were waited for; matrix products, arithmetic and copies ran while one was open for 6% of the time, Pallas kernels for 0%

commit v1 on v0

--- a/solution.py
+++ b/solution.py
@@ -4,6 +4,19 @@
 from jax.sharding import PartitionSpec as P
 
 NEGATIVE = -1e30
+
+
+def gather_around(shard, axis, dim):
+    ways = lax.axis_size(axis)
+    up = [(d, (d + 1) % ways) for d in range(ways)]
+    down = [(d, (d - 1) % ways) for d in range(ways)]
+    earlier, later = ([shard], [shard])
+    for _ in range(ways // 2):
+        earlier.append(lax.ppermute(earlier[-1], axis, up))
+    for _ in range((ways - 1) // 2):
+        later.append(lax.ppermute(later[-1], axis, down))
+    line = jnp.concatenate([*earlier[::-1], *later[1:]], axis=dim)
+    return jnp.roll(line, (lax.axis_index(axis) - ways // 2) * shard.shape[dim], axis=dim)
 
 
 def joined(part, axis, combine):
@@ -84,12 +97,7 @@
     limits = lengths[:, None] - drafts + 1 + lax.broadcasted_iota(jnp.int32, (1, drafts), 1)
     own_queries = absorb(query_nope, query_rope, key_weight)
     maxima, totals, partials = shard_partial(
-        lax.all_gather(own_queries, "seq", axis=2, tiled=True),
-        latent_cache,
-        limits,
-        offset,
-        factor,
-        latent_width,
+        gather_around(own_queries, "seq", 2), latent_cache, limits, offset, factor, latent_width
     )
     partials, maxima, totals = (partials, maxima, totals)
     sources = (partials[None], maxima[None], totals[None])

time: 213 us -> 201 us (0.944)
  waiting for transfers between devices: 138 us -> 105 us
  starting transfers between devices: 10.4 us -> 30.8 us
    all_gather x1 -> x0, waiting for transfers between devices: 44.5 us -> none  [shards(): lax.all_gather(own_queries, 'seq', axis=2, tiled=True)]
    ppermute x0 -> x7, starting transfers between devices: none -> 18.3 us  [the longest x3 12 us: gather_around(): later.append(lax.ppermute(later[-1], axis, down))]
    ppermute x0 -> x7, waiting for transfers between devices: none -> 17.7 us  [the longest x4 17.7 us: gather_around(): earlier.append(lax.ppermute(earlier[-1], axis, up))]
    all_to_all x1, waiting for transfers between devices: 16.5 us -> 11.1 us  [shards(): lax.all_to_all(sources[0].astype(jnp.float32), 'seq', split_axis=3, conca...]
    all_to_all x1, waiting for transfers between devices: 5.53 us -> 2.73 us  [shards(): lax.all_to_all(sources[2], 'seq', split_axis=3, concat_axis=0, tiled=True)]
    all_to_all x1, waiting for transfers between devices: 2.53 us -> 5.06 us  [shards(): lax.all_to_all(sources[1], 'seq', split_axis=3, concat_axis=0, tiled=True)]
    all_to_all x1, starting transfers between devices: 3.31 us -> 5.53 us  [shards(): lax.all_to_all(sources[1], 'seq', split_axis=3, concat_axis=0, tiled=True)]
    unnamed x13 -> x28, local copies, waits for them, and re-layouts: 10.2 us -> 11.3 us
  transfers between devices with their start and end apart: 6 -> 12, of which waited for: 6 -> 9; matrix products, arithmetic and copies ran while one was open for 6% -> 6% of each run, Pallas kernels for 0% -> 0%
where the time goes in v1:
time: 201 us; the launch traced here: 200 us
  waiting for transfers between devices  105 us (52%)
  starting transfers between devices  30.8 us (15%)
  local copies, waits for them, and re-layouts  19.8 us (10%)
  between operations  13.7 us (7%)
  blocking collectives  10.6 us (5%)
  other arithmetic  9.85 us (5%)
  matrix products  9.81 us (5%)
    unnamed x3, waiting for transfers between devices  63.9 us
    ppermute x4, waiting for transfers between devices, gather_around(): earlier.append(lax.ppermute(earlier[-1], axis, up))  17.7 us
    ppermute x3, starting transfers between devices, gather_around(): later.append(lax.ppermute(later[-1], axis, down))  12 us
    unnamed x28, local copies, waits for them, and re-layouts  11.3 us
    all_to_all x1, waiting for transfers between devices, shards(): lax.all_to_all(sources[0].astype(jnp.float32), 'seq', split_axis=3, conca...  11.1 us
    all_gather x2, blocking collectives, joined(): gathered = jax.tree.map(lambda a: lax.all_gather(a, axis), part)  10.6 us
    ppermute x4, starting transfers between devices, gather_around(): earlier.append(lax.ppermute(earlier[-1], axis, up))  6.29 us
    all_to_all x1, starting transfers between devices, shards(): lax.all_to_all(sources[1], 'seq', split_axis=3, concat_axis=0, tiled=True)  5.53 us
  transfers between devices with their start and end apart: 12, of which 9 were waited for; matrix products, arithmetic and copies ran while one was open for 6% of the time, Pallas kernels for 0%

profile of v1, /device:TPU:0, one launch (start us, length us, event | category | flops | bytes accessed | tf_op | source)
XLA Modules:
  0.0 200.0 jit_solution(7288513586070747988)
XLA Ops:
  8.1 1.1 fusion.18
  9.4 3.0 %collective-permute-start = (bf16[4,2,16,576]{3,0,1,2:T(4,128)(2,1)S(1)}, bf16[4,2,16,576]{3,0,1,2:T(4,128)(2,1)S(1)}, u32[]{:S(2)}, u32[]{:S(2)}) collective-permute-start(bf16[4,2,16,576]{3,0,1,2:T(4,128)(2,1)S(1)} %pad_maximum_fusion), channel_id=1, source_target_pairs={{0,4},{4,8},{8,12},{12,16},{16,20},{20,24},{24,28},{28,0},{1,5},{5... | collective-permute-start | bytes 442376 | tf_op jit(solution)/shard_map/ppermute | solution.py:15
  12.4 3.1 %collective-permute-start.4 = (bf16[4,2,16,576]{3,0,1,2:T(4,128)(2,1)S(1)}, bf16[4,2,16,576]{3,0,1,2:T(4,128)(2,1)S(1)}, u32[]{:S(2)}, u32[]{:S(2)}) collective-permute-start(bf16[4,2,16,576]{3,0,1,2:T(4,128)(2,1)S(1)} %pad_maximum_fusion), channel_id=1, source_target_pairs={{0,28},{4,0},{8,4},{12,8},{16,12},{20,16},{24,20},{28,24},{1,29},{... | collective-permute-start | bytes 442376 | tf_op jit(solution)/shard_map/ppermute | solution.py:17
  15.5 4.2 %collective-permute-done = bf16[4,2,16,576]{3,0,1,2:T(4,128)(2,1)S(1)} collective-permute-done((bf16[4,2,16,576]{3,0,1,2:T(4,128)(2,1)S(1)}, bf16[4,2,16,576]{3,0,1,2:T(4,128)(2,1)S(1)}, u32[]{:S(2)}, u32[]{:S(2)}) %collective-permute-start) | collective-permute-done | bytes 147488 | tf_op jit(solution)/shard_map/ppermute | solution.py:15
  19.8 2.1 %collective-permute-start.1 = (bf16[4,2,16,576]{3,0,1,2:T(4,128)(2,1)S(1)}, bf16[4,2,16,576]{3,0,1,2:T(4,128)(2,1)S(1)}, u32[]{:S(2)}, u32[]{:S(2)}) collective-permute-start(bf16[4,2,16,576]{3,0,1,2:T(4,128)(2,1)S(1)} %collective-permute-done), channel_id=1, source_target_pairs={{0,4},{4,8},{8,12},{12,16},{16,20},{20,24},{24,28},{28,0},{1,5},{5... | collective-permute-start | bytes 442376 | tf_op jit(solution)/shard_map/ppermute | solution.py:15
  21.9 7.0 %collective-permute-done.1 = bf16[4,2,16,576]{3,0,1,2:T(4,128)(2,1)S(1)} collective-permute-done((bf16[4,2,16,576]{3,0,1,2:T(4,128)(2,1)S(1)}, bf16[4,2,16,576]{3,0,1,2:T(4,128)(2,1)S(1)}, u32[]{:S(2)}, u32[]{:S(2)}) %collective-permute-start.1) | collective-permute-done | bytes 147488 | tf_op jit(solution)/shard_map/ppermute | solution.py:15
  29.0 4.7 %collective-permute-start.5 = (bf16[4,2,16,576]{3,0,1,2:T(4,128)(2,1)S(1)}, bf16[4,2,16,576]{3,0,1,2:T(4,128)(2,1)S(1)}, u32[]{:S(2)}, u32[]{:S(2)}) collective-permute-start(bf16[4,2,16,576]{3,0,1,2:T(4,128)(2,1)S(1)} %collective-permute-done.4), channel_id=1, source_target_pairs={{0,28},{4,0},{8,4},{12,8},{16,12},{20,16},{24,20},{28,24},{1,29},{... | collective-permute-start | bytes 442376 | tf_op jit(solution)/shard_map/ppermute | solution.py:17
  33.7 3.3 %collective-permute-done.2 = bf16[4,2,16,576]{3,0,1,2:T(4,128)(2,1)S(1)} collective-permute-done((bf16[4,2,16,576]{3,0,1,2:T(4,128)(2,1)S(1)}, bf16[4,2,16,576]{3,0,1,2:T(4,128)(2,1)S(1)}, u32[]{:S(2)}, u32[]{:S(2)}) %collective-permute-start.2) | collective-permute-done | bytes 147488 | tf_op jit(solution)/shard_map/ppermute | solution.py:15
  37.0 1.1 collective-permute-start.3
  38.2 4.2 %collective-permute-start.6 = (bf16[4,2,16,576]{3,0,1,2:T(4,128)(2,1)S(1)}, bf16[4,2,16,576]{3,0,1,2:T(4,128)(2,1)S(1)}, u32[]{:S(2)}, u32[]{:S(2)}) collective-permute-start(bf16[4,2,16,576]{3,0,1,2:T(4,128)(2,1)S(1)} %collective-permute-done.5), channel_id=1, source_target_pairs={{0,28},{4,0},{8,4},{12,8},{16,12},{20,16},{24,20},{28,24},{1,29},{... | collective-permute-start | bytes 442376 | tf_op jit(solution)/shard_map/ppermute | solution.py:17
  42.4 3.2 %collective-permute-done.3 = bf16[4,2,16,576]{3,0,1,2:T(4,128)(2,1)S(1)} collective-permute-done((bf16[4,2,16,576]{3,0,1,2:T(4,128)(2,1)S(1)}, bf16[4,2,16,576]{3,0,1,2:T(4,128)(2,1)S(1)}, u32[]{:S(2)}, u32[]{:S(2)}) %collective-permute-start.3) | collective-permute-done | bytes 147488 | tf_op jit(solution)/shard_map/ppermute | solution.py:15
  49.2 5.5 %all-to-all-start = ((f32[8,1,128]{2,1,0:T(1,128)}), f32[8,1,128]{2,1,0:T(1,128)S(1)}, u32[]{:S(2)}, u32[]{:S(2)}) async-start(f32[8,1,128]{2,1,0:T(1,128)} %reshape.83), calls=%async_computation | async-start | bytes 8192 | tf_op jit(solution)/shard_map/all_to_all | solution.py:109
  56.1 5.1 %all-to-all-done = f32[8,1,128]{2,1,0:T(1,128)S(1)} async-done(((f32[8,1,128]{2,1,0:T(1,128)}), f32[8,1,128]{2,1,0:T(1,128)S(1)}, u32[]{:S(2)}, u32[]{:S(2)}) %all-to-all-start) | async-done | bytes 4128 | tf_op jit(solution)/shard_map/all_to_all | solution.py:109
  61.2 3.3 %all-to-all-start.1 = ((f32[8,1,128]{2,1,0:T(1,128)}), f32[8,1,128]{2,1,0:T(1,128)S(1)}, u32[]{:S(2)}, u32[]{:S(2)}) async-start(f32[8,1,128]{2,1,0:T(1,128)} %reshape.85), calls=%async_computation.1 | async-start | bytes 8192 | tf_op jit(solution)/shard_map/all_to_all | solution.py:110
  64.5 1.7 fusion.11
  66.2 2.1 %copy.44 = bf16[1,4,2,128,512]{4,2,1,0,3:T(2,128)(2,1)} copy(bf16[1,4,2,128,512]{4,3,2,1,0:T(8,128)(2,1)S(1)} %fusion.11) | data formatting | bytes 2097152 | tf_op jit(solution)/shard_map/convert_element_type | solution.py:107
  68.3 2.7 %all-to-all-done.1 = f32[8,1,128]{2,1,0:T(1,128)S(1)} async-done(((f32[8,1,128]{2,1,0:T(1,128)}), f32[8,1,128]{2,1,0:T(1,128)S(1)}, u32[]{:S(2)}, u32[]{:S(2)}) %all-to-all-start.1) | async-done | bytes 4128 | tf_op jit(solution)/shard_map/all_to_all | solution.py:110
  71.0 3.6 %all-to-all-start.2 = ((bf16[1,4,2,128,512]{4,2,1,0,3:T(2,128)(2,1)}), bf16[1,4,2,128,512]{4,2,1,0,3:T(2,128)(2,1)S(1)}, u32[]{:S(2)}, u32[]{:S(2)}) async-start(bf16[1,4,2,128,512]{4,2,1,0,3:T(2,128)(2,1)} %copy.44), calls=%async_computation.2 | async-start | bytes 2097152 | tf_op jit(solution)/shard_map/all_to_all | solution.py:106
  77.8 1.6 copy.41
  79.5 1.8 fusion.40
  81.3 11.1 %all-to-all-done.2 = bf16[1,4,2,128,512]{4,2,1,0,3:T(2,128)(2,1)S(1)} async-done(((bf16[1,4,2,128,512]{4,2,1,0,3:T(2,128)(2,1)}), bf16[1,4,2,128,512]{4,2,1,0,3:T(2,128)(2,1)S(1)}, u32[]{:S(2)}, u32[]{:S(2)}) %all-to-all-start.2) | async-done | bytes 1048608 | tf_op jit(solution)/shard_map/all_to_all | solution.py:106
  92.4 2.3 %fusion.7 = f32[4,2,16,512]{3,1,0,2:T(2,128)S(1)} fusion(bf16[1,4,2,8,16,512]{5,2,1,4,3,0:T(2,128)(2,1)S(1)} %bitcast.108, f32[8,4,2,16]{2,1,3,0:T(4,128)} %get-tuple-element.201), kind=kLoop, calls=%fused_computation.13 | loop fusion | flops 1507328 | bytes 1314816 | tf_op jit(solution)/shard_map/reduce_sum | solution.py:58
  96.0 5.2 %all-gather = f32[16,2,16]{2,1,0:T(2,128)S(1)} all-gather(f32[4,2,16]{2,1,0:T(2,128)S(1)} %copy.39), channel_id=2, replica_groups=mesh['seq'=8,'grp'=4] {'grp'}, dimensions={0}, use_global_device_ids=true | all-gather | bytes 2560 | tf_op jit(solution)/shard_map/all_gather | solution.py:23
  101.2 5.4 %all-gather.1 = f32[16,2,16]{2,1,0:T(2,128)S(1)} all-gather(f32[4,2,16]{2,1,0:T(2,128)S(1)} %copy.42), channel_id=3, replica_groups=mesh['seq'=8,'grp'=4] {'grp'}, dimensions={0}, use_global_device_ids=true | all-gather | bytes 2560 | tf_op jit(solution)/shard_map/all_gather | solution.py:23
  106.6 4.8 %all-gather.4.cloned.1.call-done = f32[4,4,2,16,512]{4,3,2,1,0:T(8,128)} async-done(((f32[1,4,2,16,512]{4,3,2,1,0:T(8,128)}), f32[4,4,2,16,512]{4,3,2,1,0:T(8,128)}) %all-gather.4.cloned.1.call-update) | async-done | bytes 1048592 | tf_op jit(solution)/shard_map/all_gather | solution.py:23
  112.4 3.5 %while.19 = (s32[]{:T(128)}, f32[4,2,16]{2,1,0:T(2,128)S(1)}, f32[4,2,16]{2,1,0:T(2,128)S(1)}, f32[4,2,16,512]{3,2,1,0:T(8,128)S(1)}, f32[4,4,2,16]{3,2,1,0:T(2,...) while((s32[]{:T(128)}, f32[4,2,16]{2,1,0:T(2,128)S(1)}, ...), condition=%wide.region_6.7_spmd, body=%wide.region_5.6_spmd.sunk | while | flops 262917 | bytes 792215 | solution.py:28
  112.4 1.1 fusion.46
  115.9 2.0 %fusion.24 = bf16[16,2,1,4,128]{4,3,2,1,0:T(4,128)(2,1)S(1)} fusion(bf16[16,512,128]{2,1,0:T(8,128)(2,1)} %param.14, bf16[4,2,16,512]{3,2,1,0:T(8,128)(2,1)S(1)} %convert_element_type.59), kind=kOutput, calls=%fused_computation.26 | convolution fusion | flops 16793600 | bytes 2260992 | tf_op jit(solution)/shard_map/bqhd,hde->bqhe/dot_general | solution.py:85
  117.9 4.2 %fusion.3 = f32[4,2,1792]{2,0,1:T(4,128)S(1)} fusion(bf16[2048,1792]{1,0:T(8,128)(2,1)} %param.15, bf16[16,2,1,4,128]{4,3,2,1,0:T(4,128)(2,1)S(1)} %fusion.24), kind=kOutput, calls=%fused_computation.8 | convolution fusion | flops 58720256 | bytes 7430144 | tf_op jit(solution)/shard_map/dot_general | solution.py:115
  122.1 2.3 %copy.55 = f32[4,2,1792]{0,1,2:T(2,128)} copy(f32[4,2,1792]{2,0,1:T(4,128)S(1)} %fusion.3) | data formatting | bytes 114688
  124.4 3.1 %reshape.81 = f32[1792,8]{1,0:T(8,128)} reshape(f32[1792,2,4]{2,1,0:T(2,128)} %bitcast.107) | data formatting | bytes 114688
  127.6 63.9 %reduce-scatter.4.cloned.1.call-done = f32[224,8]{1,0:T(8,128)} async-done(((f32[1792,8]{1,0:T(8,128)}), f32[224,8]{1,0:T(8,128)}) %reduce-scatter.4.cloned.1.call-update) | async-done | bytes 7184
  (66 shorter events, 16.3 us)
Async XLA Ops:
  6.5 1.6 copy-start
  6.5 15.3 %copy-start.2 = (s32[4]{0:T(128)S(1)}, s32[4]{0:T(128)}, u32[]{:S(2)}) copy-start(s32[4]{0:T(128)} %param.12) | copy-start | bytes 52
  9.4 10.4 %collective-permute-start = (bf16[4,2,16,576]{3,0,1,2:T(4,128)(2,1)S(1)}, bf16[4,2,16,576]{3,0,1,2:T(4,128)(2,1)S(1)}, u32[]{:S(2)}, u32[]{:S(2)}) collective-permute-start(bf16[4,2,16,576]{3,0,1,2:T(4,128)(2,1)S(1)} %pad_maximum_fusion), channel_id=1, source_target_pairs={{0,4},{4,8},{8,12},{12,16},{16,20},{20,24},{24,28},{28,0},{1,5},{5... | collective-permute-start | bytes 442376 | tf_op jit(solution)/shard_map/ppermute | solution.py:15
  12.4 16.6 %collective-permute-start.4 = (bf16[4,2,16,576]{3,0,1,2:T(4,128)(2,1)S(1)}, bf16[4,2,16,576]{3,0,1,2:T(4,128)(2,1)S(1)}, u32[]{:S(2)}, u32[]{:S(2)}) collective-permute-start(bf16[4,2,16,576]{3,0,1,2:T(4,128)(2,1)S(1)} %pad_maximum_fusion), channel_id=1, source_target_pairs={{0,28},{4,0},{8,4},{12,8},{16,12},{20,16},{24,20},{28,24},{1,29},{... | collective-permute-start | bytes 442376 | tf_op jit(solution)/shard_map/ppermute | solution.py:17
  19.8 9.1 %collective-permute-start.1 = (bf16[4,2,16,576]{3,0,1,2:T(4,128)(2,1)S(1)}, bf16[4,2,16,576]{3,0,1,2:T(4,128)(2,1)S(1)}, u32[]{:S(2)}, u32[]{:S(2)}) collective-permute-start(bf16[4,2,16,576]{3,0,1,2:T(4,128)(2,1)S(1)} %collective-permute-done), channel_id=1, source_target_pairs={{0,4},{4,8},{8,12},{12,16},{16,20},{20,24},{24,28},{28,0},{1,5},{5... | collective-permute-start | bytes 442376 | tf_op jit(solution)/shard_map/ppermute | solution.py:15
  28.9 8.1 %collective-permute-start.2 = (bf16[4,2,16,576]{3,0,1,2:T(4,128)(2,1)S(1)}, bf16[4,2,16,576]{3,0,1,2:T(4,128)(2,1)S(1)}, u32[]{:S(2)}, u32[]{:S(2)}) collective-permute-start(bf16[4,2,16,576]{3,0,1,2:T(4,128)(2,1)S(1)} %collective-permute-done.1), channel_id=1, source_target_pairs={{0,4},{4,8},{8,12},{12,16},{16,20},{20,24},{24,28},{28,0},{1,5},{5... | collective-permute-start | bytes 442376 | tf_op jit(solution)/shard_map/ppermute | solution.py:15
  29.0 9.2 %collective-permute-start.5 = (bf16[4,2,16,576]{3,0,1,2:T(4,128)(2,1)S(1)}, bf16[4,2,16,576]{3,0,1,2:T(4,128)(2,1)S(1)}, u32[]{:S(2)}, u32[]{:S(2)}) collective-permute-start(bf16[4,2,16,576]{3,0,1,2:T(4,128)(2,1)S(1)} %collective-permute-done.4), channel_id=1, source_target_pairs={{0,28},{4,0},{8,4},{12,8},{16,12},{20,16},{24,20},{28,24},{1,29},{... | collective-permute-start | bytes 442376 | tf_op jit(solution)/shard_map/ppermute | solution.py:17
  37.0 8.6 %collective-permute-start.3 = (bf16[4,2,16,576]{3,0,1,2:T(4,128)(2,1)S(1)}, bf16[4,2,16,576]{3,0,1,2:T(4,128)(2,1)S(1)}, u32[]{:S(2)}, u32[]{:S(2)}) collective-permute-start(bf16[4,2,16,576]{3,0,1,2:T(4,128)(2,1)S(1)} %collective-permute-done.2), channel_id=1, source_target_pairs={{0,4},{4,8},{8,12},{12,16},{16,20},{20,24},{24,28},{28,0},{1,5},{5... | collective-permute-start | bytes 442376 | tf_op jit(solution)/shard_map/ppermute | solution.py:15
  38.2 7.9 %collective-permute-start.6 = (bf16[4,2,16,576]{3,0,1,2:T(4,128)(2,1)S(1)}, bf16[4,2,16,576]{3,0,1,2:T(4,128)(2,1)S(1)}, u32[]{:S(2)}, u32[]{:S(2)}) collective-permute-start(bf16[4,2,16,576]{3,0,1,2:T(4,128)(2,1)S(1)} %collective-permute-done.5), channel_id=1, source_target_pairs={{0,28},{4,0},{8,4},{12,8},{16,12},{20,16},{24,20},{28,24},{1,29},{... | collective-permute-start | bytes 442376 | tf_op jit(solution)/shard_map/ppermute | solution.py:17
  46.3 1.3 copy-start.1
  49.2 12.0 %all-to-all-start = ((f32[8,1,128]{2,1,0:T(1,128)}), f32[8,1,128]{2,1,0:T(1,128)S(1)}, u32[]{:S(2)}, u32[]{:S(2)}) async-start(f32[8,1,128]{2,1,0:T(1,128)} %reshape.83), calls=%async_computation | async-start | bytes 8192 | tf_op jit(solution)/shard_map/all_to_all | solution.py:109
  61.2 9.9 %all-to-all-start.1 = ((f32[8,1,128]{2,1,0:T(1,128)}), f32[8,1,128]{2,1,0:T(1,128)S(1)}, u32[]{:S(2)}, u32[]{:S(2)}) async-start(f32[8,1,128]{2,1,0:T(1,128)} %reshape.85), calls=%async_computation.1 | async-start | bytes 8192 | tf_op jit(solution)/shard_map/all_to_all | solution.py:110
  71.0 21.4 %all-to-all-start.2 = ((bf16[1,4,2,128,512]{4,2,1,0,3:T(2,128)(2,1)}), bf16[1,4,2,128,512]{4,2,1,0,3:T(2,128)(2,1)S(1)}, u32[]{:S(2)}, u32[]{:S(2)}) async-start(bf16[1,4,2,128,512]{4,2,1,0,3:T(2,128)(2,1)} %copy.44), calls=%async_computation.2 | async-start | bytes 2097152 | tf_op jit(solution)/shard_map/all_to_all | solution.py:106
  74.6 36.8 %all-gather.4.cloned.1.call-start = ((), (), s32[]{:S(2)}) async-start(), calls=%async_computation.4 | async-start | bytes 1310720 | tf_op jit(solution)/shard_map/all_gather | solution.py:23
  95.7 95.7 %reduce-scatter.4.cloned.1.call-start = ((), (), s32[]{:S(2)}) async-start(), calls=%async_computation.5 | async-start | bytes 1032192
Sparse Core Ops, SparseCore 0:
  95.9 15.5 all-gather.3
  127.7 63.7 reduce-scatter.3
